TPU v7x, 128 devices: a whole 4x4x4 slice. The times are simulated.
128 devices in a mesh: dp: 4 (over y_hi, core), tp: 32 (over y_lo, x, z).
Axes of the slice: x: 4, y: 4 (y_hi: 2, y_lo: 2; y = y_hi * 2 + y_lo), z: 4, core: 2. Of those that a mesh axis runs over, the one named last changes fastest.
Arguments:
- tokens: bfloat16 [1024, 7168], P(('dp', 'tp')), may hold values from -6 to 6
- w_gate: bfloat16 [7168, 12288], P(None, 'tp'), may hold values from -0.0625 to 0.0625
- w_up: bfloat16 [7168, 12288], P(None, 'tp'), may hold values from -0.0625 to 0.0625
- w_down: bfloat16 [12288, 7168], P('tp'), may hold values from -0.0546875 to 0.0546875
- cotangent: bfloat16 [1024, 7168], P(('dp', 'tp')), may hold values from -6 to 6
Outputs:
- mixed: bfloat16 [1024, 7168], P(('dp', 'tp'))
- input_grad: bfloat16 [1024, 7168], P(('dp', 'tp'))
- gate_grad: float32 [7168, 12288], P('dp', 'tp')
- up_grad: float32 [7168, 12288], P('dp', 'tp')
- down_grad: float32 [12288, 7168], P('tp', 'dp')
All inputs are finite; a program needn't handle non-finite values.
Results may differ from a plain program's by a relative error of at most 0.0049.
Values may be sent and summed in bfloat16 or wider, within the bound.
A program may use at most 192 MiB of HBM per device.

v0:
```python
import jax
import jax.numpy as jnp
from jax import lax
from jax.sharding import Mesh
from jax.sharding import PartitionSpec as P

TP = ("tp_0", "tp_1", "tp_2")
DP_TP = ("dp", "tp_0", "tp_1", "tp_2")


def in_order(parts, dim):
    parts = jnp.moveaxis(parts, 0, dim)
    lengths = parts.shape
    return parts.reshape(*lengths[:dim], lengths[dim] * lengths[dim + 1], *lengths[dim + 2 :])


def all_blocks(shard, axes, turns):
    parts = shard
    for k in turns:
        parts = lax.all_gather(parts, axes[k])
    done = turns[::-1]
    back = [done.index(k) for k in range(len(axes))]
    parts = parts.transpose(*back, *range(len(axes), parts.ndim))
    return parts.reshape(-1, *shard.shape)


def whole_of(shard, axes, turns, dim):
    return in_order(all_blocks(shard, axes, turns), dim)


def copy_for_each(shard, axis):
    copies = jnp.broadcast_to(shard, (lax.axis_size(axis), *shard.shape))
    return lax.all_to_all(copies, axis, split_axis=0, concat_axis=0, tiled=True)


def gather_directly(shard, axis, dim):
    parts = copy_for_each(shard, axis)
    return in_order(parts, dim)


def side_by_side(arrays, axis, dim, along):
    widths = [a.shape[along] for a in arrays]
    both = jnp.concatenate(arrays, axis=along)
    filled = gather_directly(both, axis, dim)
    return tuple(jnp.split(filled, [sum(widths[:k]) for k in range(1, len(widths))], axis=along))


def right_trans(left, matrix):
    return lax.dot_general(
        left, matrix, (((1,), (1,)), ((), ())), preferred_element_type=jnp.float32
    )


def left_trans(left, right):
    return lax.dot_general(
        left, right, (((0,), (0,)), ((), ())), preferred_element_type=jnp.float32
    )


def body(tokens, w_gate, w_up, w_down, cotangent):
    gathered = whole_of(tokens, TP, (0, 1, 2), 0)
    gate = jnp.dot(gathered, w_gate, preferred_element_type=jnp.float32)
    up = jnp.dot(gathered, w_up, preferred_element_type=jnp.float32)
    sig = jax.nn.sigmoid(gate)
    act = gate * sig
    hidden = (act * up).astype(jnp.bfloat16)
    mixed = lax.psum_scatter(
        jnp.dot(hidden, w_down, preferred_element_type=jnp.float32),
        TP,
        scatter_dimension=0,
        tiled=True,
    ).astype(jnp.bfloat16)
    grad_full = lax.all_gather(cotangent, TP, axis=0, tiled=True)
    back = right_trans(grad_full, w_down)
    dgate = (back * up * sig * (1.0 + gate * (1.0 - sig))).astype(jnp.bfloat16)
    dup = (back * act).astype(jnp.bfloat16)
    input_grad = lax.psum_scatter(
        right_trans(dgate, w_gate) + right_trans(dup, w_up), TP, scatter_dimension=0, tiled=True
    ).astype(jnp.bfloat16)
    token_part, grad_part = (
        lax.all_to_all(gathered, "dp", split_axis=1, concat_axis=0, tiled=True),
        lax.all_to_all(grad_full, "dp", split_axis=1, concat_axis=0, tiled=True),
    )
    all_dgate, all_dup, all_hidden = side_by_side((dgate, dup, hidden), "dp", 0, 1)
    gate_grad = left_trans(token_part, all_dgate)
    up_grad = left_trans(token_part, all_dup)
    down_grad = left_trans(all_hidden, grad_part)
    return (mixed, input_grad, gate_grad, up_grad, down_grad)


def solution(mesh):
    split = Mesh(mesh.devices.reshape(mesh.shape["dp"], 2, 4, 4), ("dp", "tp_0", "tp_1", "tp_2"))
    return jax.shard_map(
        body,
        mesh=split,
        in_specs=(P(DP_TP, None), P(None, TP), P(None, TP), P(TP, None), P(DP_TP, None)),
        out_specs=(P(DP_TP, None), P(DP_TP, None), P("dp", TP), P("dp", TP), P(TP, "dp")),
        check_vma=False,
    )
```

profile of v0, /device:TPU:0, one launch (start us, length us, event | category | flops | bytes accessed | tf_op | source)
XLA Modules:
  0.0 611.4 jit_solution(3640415367777148817)
XLA Ops:
  7.2 5.8 all-gather
  13.0 15.2 %all-gather.1 = bf16[8,8,7168]{2,1,0:T(8,128)(2,1)} all-gather(bf16[2,8,7168]{2,1,0:T(8,128)(2,1)S(1)} %bitcast.47), channel_id=3, replica_groups=mesh['dp'=4,'tp_0'=2,'tp_1'=4,'tp_2'=4] {'tp_1'}, dimensions={0}, use_global_device_ids=true | all-gather | bytes 1146880 | tf_op jit(solution)/shard_map/all_gather | solution.py:20
  29.0 45.9 %all-gather.8.cloned.1.call-done = bf16[16,2,8,7168]{3,2,1,0:T(8,128)(2,1)} async-done(((bf16[4,2,8,7168]{3,2,1,0:T(8,128)(2,1)}), bf16[16,2,8,7168]{3,2,1,0:T(8,128)(2,1)}) %all-gather.8.cloned.1.call-update) | async-done | bytes 3670032 | tf_op jit(solution)/shard_map/all_gather | solution.py:20
  74.9 2.5 copy.22
  83.6 148.6 %all-gather.6.cloned.1.call-done = bf16[256,7168]{1,0:T(8,128)(2,1)} async-done(((bf16[8,7168]{1,0:T(8,128)(2,1)}), bf16[256,7168]{1,0:T(8,128)(2,1)}) %all-gather.6.cloned.1.call-update) | async-done | bytes 3670032 | tf_op jit(solution)/shard_map/all_gather | solution.py:73
  232.2 5.8 multiply_convert_fusion
  238.1 7.6 %fusion.7 = f32[256,7168]{1,0:T(8,128)} fusion(bf16[256,384]{1,0:T(8,128)(2,1)S(1)} %get-tuple-element.27, bf16[384,7168]{1,0:T(8,128)(2,1)} %param.8), kind=kOutput, calls=%fused_computation.15 | convolution fusion | flops 1409286144 | bytes 13041664 | tf_op jit(solution)/shard_map/dot_general | solution.py:68
  245.9 4.8 fusion.8
  250.8 5.1 convolution_add_fusion
  255.9 7.7 %all_to_all.32 = bf16[256,4,1792]{2,1,0:T(4,128)(2,1)} reshape(bf16[2,4,4,8,7168]{4,3,2,1,0:T(8,128)(2,1)} %copy-done) | data formatting | bytes 7340032 | tf_op jit(solution)/shard_map/all_to_all | solution.py:81
  263.7 4.4 copy.24
  268.0 4.8 all-to-all-start.1
  272.9 44.0 %all-to-all-done.1 = bf16[256,4,1792]{2,0,1:T(8,128)(2,1)} async-done(((bf16[256,4,1792]{2,0,1:T(8,128)(2,1)}), bf16[256,4,1792]{2,0,1:T(8,128)(2,1)}, u32[]{:S(2)}, u32[]{:S(2)}) %all-to-all-start.1) | async-done | bytes 3670048 | tf_op jit(solution)/shard_map/all_to_all | solution.py:81
  318.5 3.6 all-to-all-start
  322.1 6.0 copy.25
  328.1 23.9 %all-to-all-done = bf16[4,256,1152]{2,1,0:T(8,128)(2,1)S(1)} async-done(((bf16[4,256,1152]{2,1,0:T(8,128)(2,1)}), bf16[4,256,1152]{2,1,0:T(8,128)(2,1)S(1)}, u32[]{:S(2)}, u32[]{:S(2)}) %all-to-all-start) | async-done | bytes 2359328 | tf_op jit(solution)/shard_map/all_to_all | solution.py:33
  353.5 4.8 all-to-all-start.2
  358.2 3.9 convolution_bitcast_fusion.1
  364.3 3.9 convolution_bitcast_fusion
  370.4 31.9 %all-to-all-done.2 = bf16[256,4,1792]{0,2,1:T(8,128)(2,1)} async-done(((bf16[256,4,1792]{0,2,1:T(8,128)(2,1)}), bf16[256,4,1792]{0,2,1:T(8,128)(2,1)}, u32[]{:S(2)}, u32[]{:S(2)}) %all-to-all-start.2) | async-done | bytes 3670048 | tf_op jit(solution)/shard_map/all_to_all | solution.py:82
  402.3 6.0 copy.26
  408.3 5.4 fusion
  413.7 12.5 %reduce-scatter.3.cloned.1.call-done = f32[8,7168]{1,0:T(8,128)} async-done(((f32[256,7168]{1,0:T(8,128)}), f32[8,7168]{1,0:T(8,128)}) %reduce-scatter.3.cloned.1.call-update) | async-done | bytes 229392 | tf_op jit(solution)/shard_map/reduce_scatter | solution.py:67
  427.8 175.4 %reduce-scatter.5.cloned.1.call-done = f32[8,7168]{1,0:T(8,128)} async-done(((f32[256,7168]{1,0:T(8,128)}), f32[8,7168]{1,0:T(8,128)}) %reduce-scatter.5.cloned.1.call-update) | async-done | bytes 229392 | tf_op jit(solution)/shard_map/reduce_scatter | solution.py:77
  (32 shorter events, 17.9 us)
Async XLA Ops:
  7.2 67.7 %all-gather.8.cloned.1.call-start = ((), (), s32[]{:S(2)}) async-start(), calls=%async_computation.8 | async-start | bytes 4587520 | tf_op jit(solution)/shard_map/all_gather | solution.py:20
  28.2 204.1 %all-gather.6.cloned.1.call-start = ((), (), s32[]{:S(2)}) async-start(), calls=%async_computation.6 | async-start | bytes 3784704 | tf_op jit(solution)/shard_map/all_gather | solution.py:73
  28.9 397.3 %reduce-scatter.3.cloned.1.call-start = ((), (), s32[]{:S(2)}) async-start(), calls=%async_computation.5 | async-start | bytes 7569408 | tf_op jit(solution)/shard_map/reduce_scatter | solution.py:67
  74.8 4.2 copy-start.1
  74.8 6.4 %slice-start = ((s8[5505024]{0:T(1024)(128)(4,1)}), s8[4194304]{0:T(1024)(128)(4,1)S(1)}, s32[]{:S(2)}) async-start(s8[5505024]{0:T(1024)(128)(4,1)} %bitcast.37), calls=%async_computation.9 | async-start | bytes 8388608
  77.3 3.9 copy-start
  79.1 2.4 slice-start.1
  245.7 357.6 %reduce-scatter.5.cloned.1.call-start = ((), (), s32[]{:S(2)}) async-start(), calls=%async_computation.7 | async-start | bytes 7569408 | tf_op jit(solution)/shard_map/reduce_scatter | solution.py:77
  245.9 4.8 slice-start.2
  245.9 4.8 slice-start.3
  268.0 48.9 %all-to-all-start.1 = ((bf16[256,4,1792]{2,0,1:T(8,128)(2,1)}), bf16[256,4,1792]{2,0,1:T(8,128)(2,1)}, u32[]{:S(2)}, u32[]{:S(2)}) async-start(bf16[256,4,1792]{2,0,1:T(8,128)(2,1)} %copy.24), calls=%async_computation.3 | async-start | bytes 7340032 | tf_op jit(solution)/shard_map/all_to_all | solution.py:81
  318.5 33.6 %all-to-all-start = ((bf16[4,256,1152]{2,1,0:T(8,128)(2,1)}), bf16[4,256,1152]{2,1,0:T(8,128)(2,1)S(1)}, u32[]{:S(2)}, u32[]{:S(2)}) async-start(bf16[4,256,1152]{2,1,0:T(8,128)(2,1)} %broadcast_in_dim.3), calls=%async_computation.2 | async-start | bytes 4718592 | tf_op jit(solution)/shard_map/all_to_all | solution.py:33
  352.1 1.4 copy-start.2
  353.5 48.8 %all-to-all-start.2 = ((bf16[256,4,1792]{0,2,1:T(8,128)(2,1)}), bf16[256,4,1792]{0,2,1:T(8,128)(2,1)}, u32[]{:S(2)}, u32[]{:S(2)}) async-start(bf16[256,4,1792]{0,2,1:T(8,128)(2,1)} %bitcast.36), calls=%async_computation.4 | async-start | bytes 7340032 | tf_op jit(solution)/shard_map/all_to_all | solution.py:82
Sparse Core Ops, SparseCore 0:
  28.3 46.5 all-gather.7
  76.5 155.7 all-gather.5
  245.8 180.3 reduce-scatter.2
  428.5 174.6 reduce-scatter.4
where the time goes:
time: 612 us; the launch traced here: 611 us
  waiting for transfers between devices  483 us (79%)
  matrix products  40.9 us (7%)
  local copies, waits for them, and re-layouts  35.8 us (6%)
  blocking collectives  20.9 us (3%)
  between operations  13.9 us (2%)
  starting transfers between devices  13.5 us (2%)
    reduce_scatter x1, waiting for transfers between devices, body(): lax.psum_scatter(right_trans(dgate, w_gate) + right_trans(dup, w_up), TP,...  175 us
    all_gather x1, waiting for transfers between devices, body(): grad_full = lax.all_gather(cotangent, TP, axis=0, tiled=True)  149 us
    all_gather x1, waiting for transfers between devices, all_blocks(): parts = lax.all_gather(parts, axes[k])  45.9 us
    all_to_all x1, waiting for transfers between devices, body(): lax.all_to_all(gathered, 'dp', split_axis=1, concat_axis=0, tiled=True)  44 us
    all_to_all x1, waiting for transfers between devices, body(): lax.all_to_all(grad_full, 'dp', split_axis=1, concat_axis=0, tiled=True)  31.9 us
    all_to_all x1, waiting for transfers between devices, copy_for_each(): return lax.all_to_all(copies, axis, split_axis=0, concat_axis=0, tiled=True)  23.9 us
    all_gather x2, blocking collectives, all_blocks(): parts = lax.all_gather(parts, axes[k])  20.9 us
    dot_general x3, matrix products, right_trans(): lax.dot_general(left, matrix, (((1,), (1,)), ((), ())), preferred_element...  15.8 us
  transfers between devices with their start and end apart: 7, of which 7 were waited for; matrix products, arithmetic and copies ran while one was open for 9% of the time, Pallas kernels for 0%

commit v1 on v0

v1 whole, which is shorter than its diff:
```python
import functools

import jax
import jax.numpy as jnp
from jax import lax
from jax.experimental import pallas as pl
from jax.experimental.pallas import tpu as pltpu
from jax.sharding import Mesh
from jax.sharding import PartitionSpec as P

TP = ("yl", "x", "z")
DP = ("yh", "co")
DP_TP = DP + TP
BF = jnp.bfloat16
F32 = jnp.float32

D = 7168
DB = 1792
H = 384
T = 1024
CH = 256
HC = 128

KIDS = {0: ((1, 1), (3, -1)), 1: ((2, 1),), 2: (), 3: ()}
IJ = (
    (0, 0),
    (1, 0), (0, 1), (3, 0), (0, 3),
    (2, 0), (1, 1), (3, 1), (1, 3), (0, 2), (3, 3),
    (2, 1), (1, 2), (3, 2), (2, 3),
    (2, 2),
)
KEPT = tuple(ij for ij in IJ if ij[1] < 2)
OI = {ij: n for n, ij in enumerate(IJ)}


def kernel(
    tok_in, cot_in, wg, wu, wd,
    sgu, sdg, yor,
    tok, cot, yin, big, wgu, wdn, gf, rb, xs, rl, yr, bf, rbb, xsb, rlb, yrb,
    sa, sd, hid, dgu, par, keep, rin, yse,
    ysend, yrecv, gsend, grecv, wsem, d1s, d1r, e1s, e1r, e2s, e2r,
    d2s, d2r, rsend, rrecv, fsend, frecv,
):
    yh, co, yl = lax.axis_index("yh"), lax.axis_index("co"), lax.axis_index("yl")
    x, z = lax.axis_index("x"), lax.axis_index("z")
    y = yh * 2 + yl
    f = y * 2 + co
    d = yh * 2 + co

    def ring_dev(g):
        gy = g // 2
        return {"yh": gy // 2, "yl": gy % 2, "co": g % 2}

    def y_dev(k):
        gy = (y + k) % 4
        return {"yh": gy // 2, "yl": gy % 2}

    def xz_dev(c, axis, way):
        s = (1 - 2 * (c % 2)) * way
        o = c // 2
        on_x = (1 - o) if axis == 0 else o
        return {"x": (x + s * on_x + 4) % 4, "z": (z + s * (1 - on_x) + 4) % 4}

    other = {"co": 1 - co}

    def rc(src, dst, ss, rs, dev):
        return pltpu.make_async_remote_copy(
            src_ref=src, dst_ref=dst, send_sem=ss, recv_sem=rs,
            device_id=dev, device_id_type=pl.DeviceIdType.MESH,
        )

    def got(dst, rs):
        rc(dst, dst, rs, rs, other).wait_recv()

    def sent(src, ss):
        rc(src, src, ss, ss, other).wait_send()

    w_copies = (
        pltpu.make_async_copy(wg.at[pl.ds(d * DB, DB), :], wgu.at[:, pl.ds(0, H)], wsem.at[0]),
        pltpu.make_async_copy(wu.at[pl.ds(d * DB, DB), :], wgu.at[:, pl.ds(H, H)], wsem.at[1]),
        pltpu.make_async_copy(wd.at[:, pl.ds(d * DB, DB)], wdn, wsem.at[2]),
    )
    in_copies = (
        pltpu.make_async_copy(tok_in, tok, wsem.at[3]),
        pltpu.make_async_copy(cot_in, cot, wsem.at[4]),
    )
    for cp in in_copies + w_copies:
        cp.start()

    barrier = pltpu.get_barrier_semaphore()
    for dev in ({"x": (x + 1) % 4}, {"x": (x + 3) % 4}, {"z": (z + 1) % 4}, {"z": (z + 3) % 4}):
        pl.semaphore_signal(barrier, inc=1, device_id=dev, device_id_type=pl.DeviceIdType.MESH)
    for k in range(1, 8):
        pl.semaphore_signal(
            barrier, inc=1, device_id=ring_dev((f + k) % 8), device_id_type=pl.DeviceIdType.MESH
        )
    pl.semaphore_wait(barrier, 11)

    for a, src in ((0, tok), (1, cot)):
        in_copies[a].wait()

        @pl.loop(0, 7)
        def _(n):
            k = (n + 1) // 2
            g = ((y + k + (k // 2) * (1 - 2 * (k // 3))) % 4) * 2 + (co + n + 1) % 2
            gd = (g // 4) * 2 + g % 2
            rc(
                src.at[:, pl.ds(pl.multiple_of(gd * DB, 128), DB)], yin.at[a, f],
                ysend.at[a, g], yrecv.at[a, f], ring_dev(g),
            ).start()
    for a, src in ((0, tok), (1, cot)):
        yin[a, f] = src[:, pl.ds(pl.multiple_of(d * DB, 128), DB)]

    def rows(oi, c):
        return pl.ds(pl.multiple_of(oi * 64 + c * 16, 16), 16)

    def near(n):
        return (y + n + (n // 2) * (1 - 2 * (n // 3))) % 4

    def along_second(a, oi, c):
        i, j = IJ[oi]
        src = big.at[a, rows(oi, c)]
        for kid, way in KIDS[j]:
            to = OI[i, kid]
            rc(src, big.at[a, rows(to, c)], gsend.at[a, to, c], grecv.at[a, to, c],
               xz_dev(c, 1, way)).start()

    def gather_step(a, oi):
        i, j = IJ[oi]

        @pl.loop(0, 4)
        def _(n):
            if oi == 0:
                c = near(n)
                halves = []
                for h in range(2):
                    g = c * 2 + h

                    @pl.when(g != f)
                    def _():
                        got(yin.at[a, g], yrecv.at[a, g])

                    halves.append(yin[a, g].astype(F32))
                big[a, rows(0, c), :] = jnp.concatenate(halves, axis=0).astype(BF)
            else:
                c = n
                got(big.at[a, rows(oi, c)], grecv.at[a, oi, c])
            src = big.at[a, rows(oi, c)]
            if j == 0:
                for kid, way in KIDS[i]:
                    to = OI[kid, 0]
                    rc(src, big.at[a, rows(to, c)], gsend.at[a, to, c], grecv.at[a, to, c],
                       xz_dev(c, 0, way)).start()
            if oi:
                along_second(a, oi, c)

        if oi == 0:
            @pl.loop(0, 4)
            def _(n):
                along_second(a, oi, near(n))

    mine = HC * co
    theirs = HC - mine

    def half_rows(k, off):
        return pl.ds(pl.multiple_of(k * CH + off, HC), HC)

    part = ((gf, rb, xs, rl, yr), (bf, rbb, xsb, rlb, yrb))

    def product(a, k):
        full = part[a][0]
        left = big.at[a, pl.ds(k * CH, CH)]
        if a == 0:
            if k == 0:
                w_copies[0].wait()
                w_copies[1].wait()

            @pl.loop(0, 3)
            def _(n):
                cols = pl.ds(pl.multiple_of(n * 256, 256), 256)
                full[pl.ds(k * CH, CH), cols] = jnp.dot(
                    left[...], wgu[:, cols], preferred_element_type=F32
                )
        else:
            if k == 0:
                w_copies[2].wait()
            full[pl.ds(k * CH, CH), :] = lax.dot_general(
                left[...], wdn[...], (((1,), (1,)), ((), ())), preferred_element_type=F32
            )
        rc(full.at[half_rows(k, theirs)], part[a][1].at[k], d1s.at[a, k], d1r.at[a, k], other).start()

    def chip_sum(a, k):
        full, recv, out, relay, _ = part[a]
        got(recv.at[k], d1r.at[a, k])
        s = full[half_rows(k, mine), :] + recv[k]
        full[half_rows(k, mine), :] = s
        out[k] = s.astype(BF)
        for w, way in ((0, 1), (1, -1)):
            rc(out.at[k, pl.ds(w * 64, 64)], relay.at[k, w], e1s.at[a, k, w], e1r.at[a, k, w],
               y_dev(way + 4)).start()

    def relay_on(a, k):
        _, _, _, relay, recv = part[a]
        for w, way in ((0, 1), (1, -1)):
            got(relay.at[k, w], e1r.at[a, k, w])
            rc(relay.at[k, w], recv.at[k, pl.ds(w * 64, 64)], e2s.at[a, k, w], e2r.at[a, k, w],
               y_dev(way + 4)).start()

    def total(a, k, cols):
        full, _, _, _, recv = part[a]
        return full[half_rows(k, mine), cols] + recv[k, :, cols].astype(F32)

    def arrived(a, k):
        recv = part[a][4]
        for w in range(2):
            got(recv.at[k, pl.ds(w * 64, 64)], e2r.at[a, k, w])

    def forward_act(k):
        arrived(0, k)
        gate = total(0, k, pl.ds(0, H))
        up = total(0, k, pl.ds(H, H))
        sig = 1.0 / (1.0 + jnp.exp(-gate))
        act = gate * sig
        sa[pl.ds(k * HC, HC), :] = act
        sd[pl.ds(k * HC, HC), :] = up * sig * (1.0 + gate * (1.0 - sig))
        hid[half_rows(k, mine), :] = (act * up).astype(BF)
        rc(hid.at[half_rows(k, mine)], hid.at[half_rows(k, mine)], d2s.at[0, k], d2r.at[0, k], other).start()

    def backward_act(k):
        arrived(1, k)
        back = total(1, k, pl.ds(0, H))
        dgu[half_rows(k, mine), pl.ds(0, H)] = (back * sd[pl.ds(k * HC, HC), :]).astype(BF)
        dgu[half_rows(k, mine), pl.ds(H, H)] = (back * sa[pl.ds(k * HC, HC), :]).astype(BF)
        rc(dgu.at[half_rows(k, mine)], dgu.at[half_rows(k, mine)], d2s.at[1, k], d2r.at[1, k], other).start()

    def put(a, k, cols, r):
        for n in range(8):
            oi = 8 * k + n
            piece = r[n * 64 : n * 64 + 64]
            if IJ[oi] in KEPT:
                keep[a, pl.ds(KEPT.index(IJ[oi]) * 64, 64), cols] = piece
            else:
                par[a, pl.ds(oi * 64, 64), cols] = piece.astype(BF)

    def mixed_part(k):
        for n in (2 * k, 2 * k + 1):
            got(hid.at[half_rows(n, theirs)], d2r.at[0, n])

        @pl.loop(0, 7)
        def _(n):
            cols = pl.ds(pl.multiple_of(n * 256, 256), 256)
            put(0, k, cols, jnp.dot(
                hid[pl.ds(k * 512, 512), :], wdn[:, cols], preferred_element_type=F32
            ))

    def igrad_part(k):
        for n in (2 * k, 2 * k + 1):
            got(dgu.at[half_rows(n, theirs)], d2r.at[1, n])

        @pl.loop(0, 7)
        def _(n):
            cols = pl.ds(pl.multiple_of(n * 256, 256), 256)
            put(1, k, cols, lax.dot_general(
                dgu[pl.ds(k * 512, 512), :], wgu[cols, :], (((1,), (1,)), ((), ())),
                preferred_element_type=F32,
            ))

    def reduce_step(a, oi):
        i, j = IJ[oi]
        kids = [OI[i, kid] for kid, _ in KIDS[j]]
        if j == 0:
            kids += [OI[kid, 0] for kid, _ in KIDS[i]]
        if oi:
            if j:
                parent, axis = next(((i, p), 1) for p in KIDS for q, _ in KIDS[p] if q == j)
                way = next(w for p in KIDS for q, w in KIDS[p] if q == j)
            else:
                parent, axis = next(((p, 0), 0) for p in KIDS for q, _ in KIDS[p] if q == i)
                way = next(w for p in KIDS for q, w in KIDS[p] if q == i)

        @pl.loop(0, 4)
        def _(c):
            if kids:
                acc = keep[a, rows(KEPT.index((i, j)), c), :]
                for kid in kids:
                    got(rin.at[a, rows(kid, c)], rrecv.at[a, kid, c])
                    acc += rin[a, rows(kid, c), :].astype(F32)
                if oi:
                    par[a, rows(oi, c), :] = acc.astype(BF)
                else:
                    for h in range(2):
                        g = c * 2 + h
                        yse[a, g] = acc[h * 8 : h * 8 + 8]

                        @pl.when(g != f)
                        def _():
                            rc(yse.at[a, g], yor.at[a, f], fsend.at[a, g], frecv.at[a, f],
                               ring_dev(g)).start()
            if oi:
                rc(par.at[a, rows(oi, c)], rin.at[a, rows(oi, c)], rsend.at[a, oi, c],
                   rrecv.at[a, oi, c], xz_dev(c, axis, -way)).start()

    def finish(a):
        yor[a, f] = yse[a, f]

        @pl.loop(1, 8)
        def _(k):
            g = (f + k) % 8
            got(yor.at[a, g], frecv.at[a, g])

    def down_piece(n):
        cols = pl.ds(n * 256, 256)
        sdg[:, cols] = lax.dot_general(
            hid[...], big[1, :, cols], (((0,), (0,)), ((), ())), preferred_element_type=F32
        )

    def gate_up_piece(n):
        r = pl.ds(n * 256, 256)
        sgu[r, :] = lax.dot_general(
            big[0, :, r], dgu[...], (((0,), (0,)), ((), ())), preferred_element_type=F32
        )

    steps = {
        "T": functools.partial(gather_step, 0),
        "C": functools.partial(gather_step, 1),
        "GU": functools.partial(product, 0),
        "B": functools.partial(product, 1),
        "S": functools.partial(chip_sum, 0),
        "SB": functools.partial(chip_sum, 1),
        "R": functools.partial(relay_on, 0),
        "RB": functools.partial(relay_on, 1),
        "H": forward_act,
        "DB": backward_act,
        "M": mixed_part,
        "I": igrad_part,
        "RM": functools.partial(reduce_step, 0),
        "RI": functools.partial(reduce_step, 1),
        "WD": down_piece,
        "WG": gate_up_piece,
        "FM": finish,
        "FI": finish,
    }
    for word in PROGRAM:
        name = word.rstrip("0123456789")
        with jax.named_scope(word):
            steps[name](int(word[len(name):]))

    for a in range(2):
        @pl.loop(1, 8)
        def _(k):
            g = (f + k) % 8
            sent(yin.at[a, g], ysend.at[a, g])
            sent(yse.at[a, g], fsend.at[a, g])

        @pl.loop(4, 64)
        def _(n):
            oi, c = n // 4, n % 4
            sent(big.at[a, rows(oi, c)], gsend.at[a, oi, c])
            sent(par.at[a, rows(oi, c)], rsend.at[a, oi, c])
        for k in range(4):
            sent(part[a][1].at[k], d1s.at[a, k])
            for w in range(2):
                sent(part[a][3].at[k, w], e1s.at[a, k, w])
                sent(part[a][3].at[k, w], e2s.at[a, k, w])
            sent((hid, dgu)[a].at[half_rows(k, mine)], d2s.at[a, k])


PROGRAM = (
    "T0", "T1", "T3", "T2", "GU0", "T5", "S0", "T4", "T6", "T7", "GU1", "T10",
    "S1", "T9", "T11", "T14", "T8", "C0", "R0", "GU2", "S2", "T12", "R1", "T15",
    "T13", "GU3", "C1", "C3", "S3", "H0", "C2", "B0", "R2", "R3", "C5", "SB0",
    "H1", "H2", "C10", "C4", "C7", "C6", "B1", "M0", "H3", "RM4", "RB0", "SB1",
    "C11", "C9", "C8", "M1", "RM13", "RM12", "C13", "B2", "RM15", "C12", "RM10", "C14",
    "RM14", "SB2", "DB0", "C15", "B3", "RB1", "RM7", "SB3", "WD3", "RM9", "DB1", "RM11",
    "RM8", "RB2", "RM6", "RB3", "I0", "DB2", "RI4", "WD6", "DB3", "RM3", "RM2", "RM5",
    "I1", "RI15", "RI9", "RI12", "WD5", "WG1", "RI13", "WG6", "RI11", "WD0", "WD1", "RI14",
    "RI10", "WG5", "RI7", "RI6", "RI8", "RI5", "RM1", "WG2", "WD4", "RI3", "RI2", "WG3",
    "RI1", "WG0", "WD2", "WG4", "RM0", "RI0", "FM0", "FI1",
)


def write_out(sgu, sdg, yor, mixed, igrad, gg, ug, dg, sem):
    copies = (
        pltpu.make_async_copy(sgu.at[:, pl.ds(0, H)], gg, sem.at[0]),
        pltpu.make_async_copy(sgu.at[:, pl.ds(H, H)], ug, sem.at[1]),
        pltpu.make_async_copy(sdg, dg, sem.at[2]),
    )
    for cp in copies:
        cp.start()
    for a, out in ((0, mixed), (1, igrad)):
        for b in range(4):
            g = (b // 2) * 4 + b % 2
            out[:, pl.ds(b * DB, DB)] = (yor[a, g] + yor[a, g + 2]).astype(BF)
    for cp in copies:
        cp.wait()


def body(tokens, w_gate, w_up, w_down, cotangent):
    vmem = pl.BlockSpec(memory_space=pltpu.VMEM)
    anyw = pl.BlockSpec(memory_space=pl.ANY)
    dma = pltpu.SemaphoreType.DMA
    held = pl.pallas_call(
        kernel,
        name="ffn",
        out_shape=(
            pltpu.VMEM((DB, 2 * H), F32),
            pltpu.VMEM((H, DB), F32),
            pltpu.VMEM((2, 8, 8, DB), F32),
        ),
        in_specs=[anyw] * 5,
        out_specs=(vmem, vmem, vmem),
        scratch_shapes=[
            pltpu.VMEM((8, D), BF),
            pltpu.VMEM((8, D), BF),
            pltpu.VMEM((2, 8, 8, DB), BF),
            pltpu.VMEM((2, T, DB), BF),
            pltpu.VMEM((DB, 2 * H), BF),
            pltpu.VMEM((H, DB), BF),
            pltpu.VMEM((T, 2 * H), F32),
            pltpu.VMEM((4, HC, 2 * H), F32),
            pltpu.VMEM((4, HC, 2 * H), BF),
            pltpu.VMEM((4, 2, 64, 2 * H), BF),
            pltpu.VMEM((4, HC, 2 * H), BF),
            pltpu.VMEM((T, H), F32),
            pltpu.VMEM((4, HC, H), F32),
            pltpu.VMEM((4, HC, H), BF),
            pltpu.VMEM((4, 2, 64, H), BF),
            pltpu.VMEM((4, HC, H), BF),
            pltpu.VMEM((T // 2, H), F32),
            pltpu.VMEM((T // 2, H), F32),
            pltpu.VMEM((T, H), BF),
            pltpu.VMEM((T, 2 * H), BF),
            pltpu.VMEM((2, T, DB), BF),
            pltpu.VMEM((2, T // 2, DB), F32),
            pltpu.VMEM((2, T, DB), BF),
            pltpu.VMEM((2, 8, 8, DB), F32),
            dma((2, 8)), dma((2, 8)),
            dma((2, 16, 4)), dma((2, 16, 4)),
            dma((5,)),
            dma((2, 4)), dma((2, 4)),
            dma((2, 4, 2)), dma((2, 4, 2)),
            dma((2, 4, 2)), dma((2, 4, 2)),
            dma((2, 4)), dma((2, 4)),
            dma((2, 16, 4)), dma((2, 16, 4)),
            dma((2, 8)), dma((2, 8)),
        ],
        compiler_params=pltpu.CompilerParams(
            collective_id=0, has_side_effects=True, vmem_limit_bytes=52 * 1024 * 1024
        ),
    )(tokens, cotangent, w_gate, w_up, w_down)
    return pl.pallas_call(
        write_out,
        name="write_out",
        out_shape=(
            jax.ShapeDtypeStruct((8, D), BF),
            jax.ShapeDtypeStruct((8, D), BF),
            jax.ShapeDtypeStruct((DB, H), F32),
            jax.ShapeDtypeStruct((DB, H), F32),
            jax.ShapeDtypeStruct((H, DB), F32),
        ),
        in_specs=[vmem] * 3,
        out_specs=(vmem, vmem, anyw, anyw, anyw),
        scratch_shapes=[dma((3,))],
        compiler_params=pltpu.CompilerParams(vmem_limit_bytes=2 * 1024 * 1024),
    )(*held)


def solution(mesh):
    split = Mesh(mesh.devices.reshape(2, 2, 2, 4, 4), DP_TP)
    return jax.shard_map(
        body,
        mesh=split,
        in_specs=(P(DP_TP, None), P(None, TP), P(None, TP), P(TP, None), P(DP_TP, None)),
        out_specs=(P(DP_TP, None), P(DP_TP, None), P(DP, TP), P(DP, TP), P(TP, DP)),
        check_vma=False,
    )
```

time: 612 us -> 110 us (0.18)
  waiting for transfers between devices: 483 us -> 0 us
  Pallas kernels: 0 us -> 108 us
  matrix products: 40.9 us -> 0 us
  local copies, waits for them, and re-layouts: 35.8 us -> 0 us
  blocking collectives: 20.9 us -> 0 us
  starting transfers between devices: 13.5 us -> 0 us
  between operations: 13.9 us -> 0.64 us
    all_gather x2 -> x0, waiting for transfers between devices: 195 us -> none  [the longest x1 149 us: body(): grad_full = lax.all_gather(cotangent, TP, axis=0, tiled=True)]
    reduce_scatter x2 -> x0, waiting for transfers between devices: 188 us -> none  [the longest x1 175 us: body(): lax.psum_scatter(right_trans(dgate, w_gate) + right_trans(dup, w_up), TP,...]
    pallas_call x0 -> x2, Pallas kernels: none -> 108 us  [the longest x1 104 us: body(): pl.pallas_call(kernel, name='ffn', out_shape=(pltpu.VMEM((DB, 2 * H), F32...]
    all_to_all x3 -> x0, waiting for transfers between devices: 99.9 us -> none  [the longest x1 44 us: body(): lax.all_to_all(gathered, 'dp', split_axis=1, concat_axis=0, tiled=True)]
    dot_general x9 -> x0, matrix products: 40.9 us -> none  [the longest x3 15.8 us: right_trans(): lax.dot_general(left, matrix, (((1,), (1,)), ((), ())), preferred_element...]
    all_gather x2 -> x0, blocking collectives: 20.9 us -> none  [all_blocks(): parts = lax.all_gather(parts, axes[k])]
    all_to_all x3 -> x0, local copies, waits for them, and re-layouts: 18.1 us -> none  [the longest x2 12.1 us: body(): lax.all_to_all(gathered, 'dp', split_axis=1, concat_axis=0, tiled=True)]
    all_to_all x3 -> x0, starting transfers between devices: 13.2 us -> none  [the longest x1 4.78 us: body(): lax.all_to_all(gathered, 'dp', split_axis=1, concat_axis=0, tiled=True)]
  transfers between devices with their start and end apart: 7 -> 0, of which waited for: 7 -> 0; matrix products, arithmetic and copies ran while one was open for 9% -> 0% of each run, Pallas kernels for 0% -> 0%
where the time goes in v1:
time: 110 us; the launch traced here: 109 us
  Pallas kernels  108 us (98%)
    pallas_call x1, Pallas kernels, body(): pl.pallas_call(kernel, name='ffn', out_shape=(pltpu.VMEM((DB, 2 * H), F32...  104 us
    pallas_call x1, Pallas kernels, body(): pl.pallas_call(write_out, name='write_out', out_shape=(jax.ShapeDtypeStru...  4.06 us

profile of v1, /device:TPU:0, one launch (start us, length us, event | category | flops | bytes accessed | tf_op | source)
XLA Modules:
  0.0 109.0 jit_solution(7325792265936971514)
XLA Ops:
  0.6 104.3 %ffn.1 = (f32[1792,768]{1,0:T(8,128)S(1)}, f32[384,1792]{1,0:T(8,128)S(1)}, f32[2,8,8,1792]{3,2,1,0:T(8,128)S(1)}) custom-call(bf16[8,7168]{1,0:T(8,128)(2,1)} %tok_in.1, bf16[8,7168]{1,0:T(8,128)(2,1)} %cot_in.1, bf16[7168,384]{1,0:T(8,128)(2,1)} %wg.1, bf16[7168,384]{1,0:T(8,128)(2,1)} %wu.1, bf16[384,7168]{1,0:T(8,128)(2,1)} %wd.1), custom_call_target="tpu_custom_call" | custom-call | tf_op jit(solution)/shard_map/ffn/pallas_call | solution.py:402
  105.0 4.1 %write_out.1 = (bf16[8,7168]{1,0:T(8,128)(2,1)}, bf16[8,7168]{1,0:T(8,128)(2,1)}, f32[1792,384]{1,0:T(8,128)}, f32[1792,384]{1,0:T(8,128)}, f32[384,1792]{1,0:T(8,128)}) custom-call(f32[1792,768]{1,0:T(8,128)S(1)} %get-tuple-element.8.sgu, f32[384,1792]{1,0:T(8,128)S(1)} %get-tuple-element.9.sdg, f32[2,8,8,1792]{3,2,1,0:T(8,128)S(1)} %get-tuple-element.10.yor), custom_call_target="tpu_custom_call" | custom-call | tf_op jit(solution)/shard_map/write_out/pallas_call | solution.py:451

commit v2 on v1

--- a/solution.py
+++ b/solution.py
@@ -29,6 +29,8 @@
     (2, 1), (1, 2), (3, 2), (2, 3),
     (2, 2),
 )
+LEAVES = ((3, 3), (3, 2), (0, 3), (0, 2))
+REDUCE_SHARED = (LEAVES[:2], LEAVES[:4])
 KEPT = tuple(ij for ij in IJ if ij[1] < 2)
 OI = {ij: n for n, ij in enumerate(IJ)}
 
@@ -37,9 +39,9 @@
     tok_in, cot_in, wg, wu, wd,
     sgu, sdg, yor,
     tok, cot, yin, big, wgu, wdn, gf, rb, xs, rl, yr, bf, rbb, xsb, rlb, yrb,
-    sa, sd, hid, dgu, par, keep, rin, yse,
+    sa, sd, hid, dgu, par, keep, rin, pex, yse,
     ysend, yrecv, gsend, grecv, wsem, d1s, d1r, e1s, e1r, e2s, e2r,
-    d2s, d2r, rsend, rrecv, fsend, frecv,
+    d2s, d2r, rsend, rrecv, fsend, frecv, qsend, qrecv,
 ):
     yh, co, yl = lax.axis_index("yh"), lax.axis_index("co"), lax.axis_index("yl")
     x, z = lax.axis_index("x"), lax.axis_index("z")
@@ -62,6 +64,13 @@
         return {"x": (x + s * on_x + 4) % 4, "z": (z + s * (1 - on_x) + 4) % 4}
 
     other = {"co": 1 - co}
+    pair = {"yl": 1 - yl}
+
+    def ours(n):
+        return yl * (1 + n) + (1 - yl) * 3 * n
+
+    def its(n):
+        return (1 - yl) * (1 + n) + yl * 3 * n
 
     def rc(src, dst, ss, rs, dev):
         return pltpu.make_async_remote_copy(
@@ -106,7 +115,7 @@
             gd = (g // 4) * 2 + g % 2
             rc(
                 src.at[:, pl.ds(pl.multiple_of(gd * DB, 128), DB)], yin.at[a, f],
-                ysend.at[a, g], yrecv.at[a, f], ring_dev(g),
+                ysend.at[a], yrecv.at[a, f], ring_dev(g),
             ).start()
     for a, src in ((0, tok), (1, cot)):
         yin[a, f] = src[:, pl.ds(pl.multiple_of(d * DB, 128), DB)]
@@ -120,42 +129,46 @@
     def along_second(a, oi, c):
         i, j = IJ[oi]
         src = big.at[a, rows(oi, c)]
+
         for kid, way in KIDS[j]:
             to = OI[i, kid]
-            rc(src, big.at[a, rows(to, c)], gsend.at[a, to, c], grecv.at[a, to, c],
+            rc(src, big.at[a, rows(to, c)], gsend.at[a], grecv.at[a, to, c],
                xz_dev(c, 1, way)).start()
 
-    def gather_step(a, oi):
+    def assemble(a, c):
+        halves = []
+        for h in range(2):
+            g = c * 2 + h
+
+            @pl.when(g != f)
+            def _():
+                got(yin.at[a, g], yrecv.at[a, g])
+
+            halves.append(yin[a, g].astype(F32))
+        big[a, rows(0, c), :] = jnp.concatenate(halves, axis=0).astype(BF)
+
+    COLOURS = {"": (0, 4), "a": (0, 1), "b": (1, 4), "c": (1, 3), "d": (3, 4)}
+
+    def gather_step(a, oi, which):
         i, j = IJ[oi]
-
-        @pl.loop(0, 4)
+        @pl.loop(*COLOURS[which])
         def _(n):
+            c = near(n)
             if oi == 0:
-                c = near(n)
-                halves = []
-                for h in range(2):
-                    g = c * 2 + h
-
-                    @pl.when(g != f)
-                    def _():
-                        got(yin.at[a, g], yrecv.at[a, g])
-
-                    halves.append(yin[a, g].astype(F32))
-                big[a, rows(0, c), :] = jnp.concatenate(halves, axis=0).astype(BF)
+                assemble(a, c)
             else:
-                c = n
                 got(big.at[a, rows(oi, c)], grecv.at[a, oi, c])
             src = big.at[a, rows(oi, c)]
             if j == 0:
                 for kid, way in KIDS[i]:
                     to = OI[kid, 0]
-                    rc(src, big.at[a, rows(to, c)], gsend.at[a, to, c], grecv.at[a, to, c],
+                    rc(src, big.at[a, rows(to, c)], gsend.at[a], grecv.at[a, to, c],
                        xz_dev(c, 0, way)).start()
             if oi:
                 along_second(a, oi, c)
 
         if oi == 0:
-            @pl.loop(0, 4)
+            @pl.loop(*COLOURS[which])
             def _(n):
                 along_second(a, oi, near(n))
 
@@ -187,7 +200,7 @@
             full[pl.ds(k * CH, CH), :] = lax.dot_general(
                 left[...], wdn[...], (((1,), (1,)), ((), ())), preferred_element_type=F32
             )
-        rc(full.at[half_rows(k, theirs)], part[a][1].at[k], d1s.at[a, k], d1r.at[a, k], other).start()
+        rc(full.at[half_rows(k, theirs)], part[a][1].at[k], d1s.at[a], d1r.at[a, k], other).start()
 
     def chip_sum(a, k):
         full, recv, out, relay, _ = part[a]
@@ -196,14 +209,14 @@
         full[half_rows(k, mine), :] = s
         out[k] = s.astype(BF)
         for w, way in ((0, 1), (1, -1)):
-            rc(out.at[k, pl.ds(w * 64, 64)], relay.at[k, w], e1s.at[a, k, w], e1r.at[a, k, w],
+            rc(out.at[k, pl.ds(w * 64, 64)], relay.at[k, w], e1s.at[a], e1r.at[a, k, w],
                y_dev(way + 4)).start()
 
     def relay_on(a, k):
         _, _, _, relay, recv = part[a]
         for w, way in ((0, 1), (1, -1)):
             got(relay.at[k, w], e1r.at[a, k, w])
-            rc(relay.at[k, w], recv.at[k, pl.ds(w * 64, 64)], e2s.at[a, k, w], e2r.at[a, k, w],
+            rc(relay.at[k, w], recv.at[k, pl.ds(w * 64, 64)], e2s.at[a], e2r.at[a, k, w],
                y_dev(way + 4)).start()
 
     def total(a, k, cols):
@@ -224,14 +237,14 @@
         sa[pl.ds(k * HC, HC), :] = act
         sd[pl.ds(k * HC, HC), :] = up * sig * (1.0 + gate * (1.0 - sig))
         hid[half_rows(k, mine), :] = (act * up).astype(BF)
-        rc(hid.at[half_rows(k, mine)], hid.at[half_rows(k, mine)], d2s.at[0, k], d2r.at[0, k], other).start()
+        rc(hid.at[half_rows(k, mine)], hid.at[half_rows(k, mine)], d2s.at[0], d2r.at[0, k], other).start()
 
     def backward_act(k):
         arrived(1, k)
         back = total(1, k, pl.ds(0, H))
         dgu[half_rows(k, mine), pl.ds(0, H)] = (back * sd[pl.ds(k * HC, HC), :]).astype(BF)
         dgu[half_rows(k, mine), pl.ds(H, H)] = (back * sa[pl.ds(k * HC, HC), :]).astype(BF)
-        rc(dgu.at[half_rows(k, mine)], dgu.at[half_rows(k, mine)], d2s.at[1, k], d2r.at[1, k], other).start()
+        rc(dgu.at[half_rows(k, mine)], dgu.at[half_rows(k, mine)], d2s.at[1], d2r.at[1, k], other).start()
 
     def put(a, k, cols, r):
         for n in range(8):
@@ -246,9 +259,8 @@
         for n in (2 * k, 2 * k + 1):
             got(hid.at[half_rows(n, theirs)], d2r.at[0, n])
 
-        @pl.loop(0, 7)
-        def _(n):
-            cols = pl.ds(pl.multiple_of(n * 256, 256), 256)
+        for n in range(7):
+            cols = pl.ds(n * 256, 256)
             put(0, k, cols, jnp.dot(
                 hid[pl.ds(k * 512, 512), :], wdn[:, cols], preferred_element_type=F32
             ))
@@ -257,30 +269,57 @@
         for n in (2 * k, 2 * k + 1):
             got(dgu.at[half_rows(n, theirs)], d2r.at[1, n])
 
-        @pl.loop(0, 7)
-        def _(n):
-            cols = pl.ds(pl.multiple_of(n * 256, 256), 256)
+        for n in range(7):
+            cols = pl.ds(n * 256, 256)
             put(1, k, cols, lax.dot_general(
                 dgu[pl.ds(k * 512, 512), :], wgu[cols, :], (((1,), (1,)), ((), ())),
                 preferred_element_type=F32,
             ))
 
-    def reduce_step(a, oi):
+    def reduce_step(a, oi, which):
         i, j = IJ[oi]
-        kids = [OI[i, kid] for kid, _ in KIDS[j]]
+        kids = [OI[i, kid] for kid, _ in KIDS[j] if (i, kid) not in REDUCE_SHARED[a]]
         if j == 0:
             kids += [OI[kid, 0] for kid, _ in KIDS[i]]
         if oi:
-            if j:
-                parent, axis = next(((i, p), 1) for p in KIDS for q, _ in KIDS[p] if q == j)
-                way = next(w for p in KIDS for q, w in KIDS[p] if q == j)
-            else:
-                parent, axis = next(((p, 0), 0) for p in KIDS for q, _ in KIDS[p] if q == i)
-                way = next(w for p in KIDS for q, w in KIDS[p] if q == i)
-
-        @pl.loop(0, 4)
-        def _(c):
-            if kids:
+            along = j or i
+            parent, way = next((p, w) for p in KIDS for q, w in KIDS[p] if q == along)
+            above, axis = ((i, parent), 1) if j else ((parent, 0), 0)
+
+        def send(c):
+            rc(par.at[a, rows(oi, c)], rin.at[a, rows(oi, c)], rsend.at[a],
+               rrecv.at[a, oi, c], xz_dev(c, axis, -way)).start()
+
+        if which:
+            leaf = LEAVES.index((i, j)) if (i, j) in LEAVES else None
+        if which == "y":
+            @pl.loop(0, 2)
+            def _(n):
+                rc(par.at[a, rows(oi, its(n))], pex.at[a, leaf, n], qsend.at[a],
+                   qrecv.at[a, leaf, n], pair).start()
+            return
+        if which == "x":
+            @pl.loop(0, 2)
+            def _(n):
+                c = ours(n)
+                got(pex.at[a, leaf, n], qrecv.at[a, leaf, n])
+                par[a, rows(oi, c), :] = (
+                    par[a, rows(oi, c), :].astype(F32) + pex[a, leaf, n].astype(F32)
+                ).astype(BF)
+                send(c)
+            return
+        if which == "k":
+            @pl.loop(0, 2)
+            def _(n):
+                c = ours(n)
+                got(rin.at[a, rows(oi, c)], rrecv.at[a, oi, c])
+                keep[a, rows(KEPT.index(above), c), :] += rin[a, rows(oi, c), :].astype(F32)
+            return
+
+        @pl.loop(*COLOURS[which])
+        def _(n):
+            c = near(3 - n) if which == "" else near(n)
+            if (i, j) in KEPT:
                 acc = keep[a, rows(KEPT.index((i, j)), c), :]
                 for kid in kids:
                     got(rin.at[a, rows(kid, c)], rrecv.at[a, kid, c])
@@ -294,11 +333,10 @@
 
                         @pl.when(g != f)
                         def _():
-                            rc(yse.at[a, g], yor.at[a, f], fsend.at[a, g], frecv.at[a, f],
+                            rc(yse.at[a, g], yor.at[a, f], fsend.at[a], frecv.at[a, f],
                                ring_dev(g)).start()
             if oi:
-                rc(par.at[a, rows(oi, c)], rin.at[a, rows(oi, c)], rsend.at[a, oi, c],
-                   rrecv.at[a, oi, c], xz_dev(c, axis, -way)).start()
+                send(c)
 
     def finish(a):
         yor[a, f] = yse[a, f]
@@ -341,56 +379,58 @@
         "FI": finish,
     }
     for word in PROGRAM:
-        name = word.rstrip("0123456789")
+        name = word.rstrip("abcdkxy").rstrip("0123456789")
+        number = word[len(name):].rstrip("abcdkxy")
+        which = word[len(name) + len(number):]
         with jax.named_scope(word):
-            steps[name](int(word[len(name):]))
+            if name in ("T", "C", "RM", "RI"):
+                steps[name](int(number), which)
+            else:
+                steps[name](int(number))
 
     for a in range(2):
-        @pl.loop(1, 8)
-        def _(k):
-            g = (f + k) % 8
-            sent(yin.at[a, g], ysend.at[a, g])
-            sent(yse.at[a, g], fsend.at[a, g])
-
-        @pl.loop(4, 64)
-        def _(n):
-            oi, c = n // 4, n % 4
-            sent(big.at[a, rows(oi, c)], gsend.at[a, oi, c])
-            sent(par.at[a, rows(oi, c)], rsend.at[a, oi, c])
-        for k in range(4):
-            sent(part[a][1].at[k], d1s.at[a, k])
-            for w in range(2):
-                sent(part[a][3].at[k, w], e1s.at[a, k, w])
-                sent(part[a][3].at[k, w], e2s.at[a, k, w])
-            sent((hid, dgu)[a].at[half_rows(k, mine)], d2s.at[a, k])
+        sent(yin.at[a, pl.ds(0, 7)], ysend.at[a])
+        sent(big.at[a, pl.ds(0, 15 * 64)], gsend.at[a])
+        sent(part[a][1], d1s.at[a])
+        sent(part[a][3], e1s.at[a])
+        sent(part[a][3], e2s.at[a])
+        sent((hid, dgu)[a].at[pl.ds(0, T // 2)], d2s.at[a])
+        shared = len(REDUCE_SHARED[a])
+        sent(pex.at[a, pl.ds(0, shared)], qsend.at[a])
+        sent(par.at[a, pl.ds(0, 15 * 64 - 32 * shared)], rsend.at[a])
+        sent(yse.at[a, pl.ds(0, 7)], fsend.at[a])
 
 
 PROGRAM = (
-    "T0", "T1", "T3", "T2", "GU0", "T5", "S0", "T4", "T6", "T7", "GU1", "T10",
-    "S1", "T9", "T11", "T14", "T8", "C0", "R0", "GU2", "S2", "T12", "R1", "T15",
-    "T13", "GU3", "C1", "C3", "S3", "H0", "C2", "B0", "R2", "R3", "C5", "SB0",
-    "H1", "H2", "C10", "C4", "C7", "C6", "B1", "M0", "H3", "RM4", "RB0", "SB1",
-    "C11", "C9", "C8", "M1", "RM13", "RM12", "C13", "B2", "RM15", "C12", "RM10", "C14",
-    "RM14", "SB2", "DB0", "C15", "B3", "RB1", "RM7", "SB3", "WD3", "RM9", "DB1", "RM11",
-    "RM8", "RB2", "RM6", "RB3", "I0", "DB2", "RI4", "WD6", "DB3", "RM3", "RM2", "RM5",
-    "I1", "RI15", "RI9", "RI12", "WD5", "WG1", "RI13", "WG6", "RI11", "WD0", "WD1", "RI14",
-    "RI10", "WG5", "RI7", "RI6", "RI8", "RI5", "RM1", "WG2", "WD4", "RI3", "RI2", "WG3",
-    "RI1", "WG0", "WD2", "WG4", "RM0", "RI0", "FM0", "FI1",
+    "T0a", "T0c", "T4a", "T0d", "T1a", "T2a", "T3a", "T1b", "T3b", "T2b", "GU0", "T5",
+    "T6", "S0", "T4b", "T7", "GU1", "T10", "S1", "T9", "T8", "T11", "GU2", "T14",
+    "C0", "R0", "T12", "S2", "T13", "R1", "T15", "GU3", "H0", "C3", "S3", "C1",
+    "C2", "R2", "H1", "B0", "R3", "M0", "RM4", "SB0", "C5", "C7", "C4", "C6",
+    "B1", "H2", "H3", "C9", "SB1", "RB0", "C10", "M1", "RM10y", "C11", "RM15", "RM13y",
+    "RM12", "C14", "RM9", "C13", "RM14", "RB1", "C12", "C8", "DB0", "B2", "C15", "B3",
+    "SB2", "RM11", "SB3", "RM6", "DB1", "RM13x", "RB2", "RM8", "WD0", "RB3", "RM5", "RM10x",
+    "I0", "DB2", "RM2", "DB3", "RM13k", "RM7", "RI4y", "RM1", "I1", "RI15", "RI13y", "WD4",
+    "RI9y", "RI12", "RM10k", "RM3", "RI14", "RI10y", "WG3", "WD5", "RI11", "RI6", "WD2", "RI13x",
+    "RI8", "RM0", "RI4x", "RI9x", "WG5", "RI5b", "WD1", "RI10x", "WG4", "RI13k", "RI7", "WD3",
+    "RI4k", "RI5a", "WD6", "RI9k", "RI2b", "RI2a", "RI1b", "RI10k", "RI3b", "WG2", "RI1a", "RI0d",
+    "WG1", "RI0c", "FM0", "RI3a", "WG0", "RI0a", "WG6", "FI1",
 )
 
 
-def write_out(sgu, sdg, yor, mixed, igrad, gg, ug, dg, sem):
-    copies = (
+def write_out(sgu, sdg, yor, mixed, igrad, gg, ug, dg, rows, sem):
+    copies = [
         pltpu.make_async_copy(sgu.at[:, pl.ds(0, H)], gg, sem.at[0]),
         pltpu.make_async_copy(sgu.at[:, pl.ds(H, H)], ug, sem.at[1]),
         pltpu.make_async_copy(sdg, dg, sem.at[2]),
-    )
+    ]
     for cp in copies:
         cp.start()
     for a, out in ((0, mixed), (1, igrad)):
         for b in range(4):
             g = (b // 2) * 4 + b % 2
-            out[:, pl.ds(b * DB, DB)] = (yor[a, g] + yor[a, g + 2]).astype(BF)
+            rows[a, :, pl.ds(b * DB, DB)] = (yor[a, g] + yor[a, g + 2]).astype(BF)
+        copies.append(pltpu.make_async_copy(rows.at[a], out, sem.at[3 + a]))
+        copies[-1].start()
     for cp in copies:
         cp.wait()
 
@@ -433,19 +473,21 @@
             pltpu.VMEM((2, T, DB), BF),
             pltpu.VMEM((2, T // 2, DB), F32),
             pltpu.VMEM((2, T, DB), BF),
+            pltpu.VMEM((2, 4, 2, 16, DB), BF),
             pltpu.VMEM((2, 8, 8, DB), F32),
-            dma((2, 8)), dma((2, 8)),
-            dma((2, 16, 4)), dma((2, 16, 4)),
+            dma((2,)), dma((2, 8)),
+            dma((2,)), dma((2, 16, 4)),
             dma((5,)),
-            dma((2, 4)), dma((2, 4)),
-            dma((2, 4, 2)), dma((2, 4, 2)),
-            dma((2, 4, 2)), dma((2, 4, 2)),
-            dma((2, 4)), dma((2, 4)),
-            dma((2, 16, 4)), dma((2, 16, 4)),
-            dma((2, 8)), dma((2, 8)),
+            dma((2,)), dma((2, 4)),
+            dma((2,)), dma((2, 4, 2)),
+            dma((2,)), dma((2, 4, 2)),
+            dma((2,)), dma((2, 4)),
+            dma((2,)), dma((2, 16, 4)),
+            dma((2,)), dma((2, 8)),
+            dma((2,)), dma((2, 4, 2)),
         ],
         compiler_params=pltpu.CompilerParams(
-            collective_id=0, has_side_effects=True, vmem_limit_bytes=52 * 1024 * 1024
+            collective_id=0, has_side_effects=True, vmem_limit_bytes=53 * 1024 * 1024
         ),
     )(tokens, cotangent, w_gate, w_up, w_down)
     return pl.pallas_call(
@@ -459,8 +501,8 @@
             jax.ShapeDtypeStruct((H, DB), F32),
         ),
         in_specs=[vmem] * 3,
-        out_specs=(vmem, vmem, anyw, anyw, anyw),
-        scratch_shapes=[dma((3,))],
+        out_specs=(anyw,) * 5,
+        scratch_shapes=[pltpu.VMEM((2, 8, D), BF), dma((5,))],
         compiler_params=pltpu.CompilerParams(vmem_limit_bytes=2 * 1024 * 1024),
     )(*held)
 

time: 110 us -> 100 us (0.909)
  Pallas kernels: 108 us -> 98.3 us
    pallas_call x1, Pallas kernels: 104 us -> 94.9 us  [body(): pl.pallas_call(kernel, name='ffn', out_shape=(pltpu.VMEM((DB, 2 * H), F32...]
where the time goes in v2:
time: 100 us; the launch traced here: 99.1 us
  Pallas kernels  98.3 us (98%)
    pallas_call x1, Pallas kernels, body(): pl.pallas_call(kernel, name='ffn', out_shape=(pltpu.VMEM((DB, 2 * H), F32...  94.9 us
    pallas_call x1, Pallas kernels, body(): pl.pallas_call(write_out, name='write_out', out_shape=(jax.ShapeDtypeStru...  3.4 us

profile of v2, /device:TPU:0, one launch (start us, length us, event | category | flops | bytes accessed | tf_op | source)
XLA Modules:
  0.0 99.1 jit_solution(13055260198644637461)
XLA Ops:
  0.6 94.9 %ffn.1 = (f32[1792,768]{1,0:T(8,128)S(1)}, f32[384,1792]{1,0:T(8,128)S(1)}, f32[2,8,8,1792]{3,2,1,0:T(8,128)S(1)}) custom-call(bf16[8,7168]{1,0:T(8,128)(2,1)} %tok_in.1, bf16[8,7168]{1,0:T(8,128)(2,1)} %cot_in.1, bf16[7168,384]{1,0:T(8,128)(2,1)} %wg.1, bf16[7168,384]{1,0:T(8,128)(2,1)} %wu.1, bf16[384,7168]{1,0:T(8,128)(2,1)} %wd.1), custom_call_target="tpu_custom_call" | custom-call | tf_op jit(solution)/shard_map/ffn/pallas_call | solution.py:442
  95.5 3.4 %write_out.1 = (bf16[8,7168]{1,0:T(8,128)(2,1)}, bf16[8,7168]{1,0:T(8,128)(2,1)}, f32[1792,384]{1,0:T(8,128)}, f32[1792,384]{1,0:T(8,128)}, f32[384,1792]{1,0:T(8,128)}) custom-call(f32[1792,768]{1,0:T(8,128)S(1)} %get-tuple-element.8.sgu, f32[384,1792]{1,0:T(8,128)S(1)} %get-tuple-element.9.sdg, f32[2,8,8,1792]{3,2,1,0:T(8,128)S(1)} %get-tuple-element.10.yor), custom_call_target="tpu_custom_call" | custom-call | tf_op jit(solution)/shard_map/write_out/pallas_call | solution.py:493

commit v3 on v2

--- a/solution.py
+++ b/solution.py
@@ -30,7 +30,7 @@
     (2, 2),
 )
 LEAVES = ((3, 3), (3, 2), (0, 3), (0, 2))
-REDUCE_SHARED = (LEAVES[:2], LEAVES[:4])
+REDUCE_SHARED = (LEAVES[:2], LEAVES[:2])
 KEPT = tuple(ij for ij in IJ if ij[1] < 2)
 OI = {ij: n for n, ij in enumerate(IJ)}
 
@@ -39,7 +39,7 @@
     tok_in, cot_in, wg, wu, wd,
     sgu, sdg, yor,
     tok, cot, yin, big, wgu, wdn, gf, rb, xs, rl, yr, bf, rbb, xsb, rlb, yrb,
-    sa, sd, hid, dgu, par, keep, rin, pex, yse,
+    sa, sd, hid, dgu, par, keep, rin, pex, yse, far_out, far_in,
     ysend, yrecv, gsend, grecv, wsem, d1s, d1r, e1s, e1r, e2s, e2r,
     d2s, d2r, rsend, rrecv, fsend, frecv, qsend, qrecv,
 ):
@@ -115,7 +115,7 @@
             gd = (g // 4) * 2 + g % 2
             rc(
                 src.at[:, pl.ds(pl.multiple_of(gd * DB, 128), DB)], yin.at[a, f],
-                ysend.at[a], yrecv.at[a, f], ring_dev(g),
+                ysend.at[a], yrecv.at[a, (k + 1) // 2], ring_dev(g),
             ).start()
     for a, src in ((0, tok), (1, cot)):
         yin[a, f] = src[:, pl.ds(pl.multiple_of(d * DB, 128), DB)]
@@ -123,6 +123,16 @@
     def rows(oi, c):
         return pl.ds(pl.multiple_of(oi * 64 + c * 16, 16), 16)
 
+    def sem_of(table, a, oi, c):
+        base, n = table[a, oi]
+        r = (c - y + 4) % 4
+        return base + (0 if n == 1 else (r + 3) // 4 if n == 2 else r - (r // 3) * 2)
+
+    def got_blocks(table, sems, buf, a, oi, which):
+        part = "acd".find(which) if which in "acd" and which else 1 if which else 0
+        lo, hi = COLOURS[which]
+        got(buf.at[a, pl.ds(oi * 64, 16 * (hi - lo))], sems.at[table[a, oi][0] + part])
+
     def near(n):
         return (y + n + (n // 2) * (1 - 2 * (n // 3))) % 4
 
@@ -132,37 +142,32 @@
 
         for kid, way in KIDS[j]:
             to = OI[i, kid]
-            rc(src, big.at[a, rows(to, c)], gsend.at[a], grecv.at[a, to, c],
+            rc(src, big.at[a, rows(to, c)], gsend.at[a], grecv.at[sem_of(GATHER_SEM, a, to, c)],
                xz_dev(c, 1, way)).start()
 
     def assemble(a, c):
-        halves = []
-        for h in range(2):
-            g = c * 2 + h
-
-            @pl.when(g != f)
-            def _():
-                got(yin.at[a, g], yrecv.at[a, g])
-
-            halves.append(yin[a, g].astype(F32))
+        halves = [yin[a, c * 2 + h].astype(F32) for h in range(2)]
         big[a, rows(0, c), :] = jnp.concatenate(halves, axis=0).astype(BF)
-
-    COLOURS = {"": (0, 4), "a": (0, 1), "b": (1, 4), "c": (1, 3), "d": (3, 4)}
 
     def gather_step(a, oi, which):
         i, j = IJ[oi]
+        if oi:
+            got_blocks(GATHER_SEM, grecv, big, a, oi, which)
+        else:
+            for part, (w, count) in enumerate((("a", 1), ("bc", 4), ("bd", 2))):
+                if which in w or not which:
+                    got(yin.at[a, pl.ds(0, count)], yrecv.at[a, part])
+
         @pl.loop(*COLOURS[which])
         def _(n):
             c = near(n)
             if oi == 0:
                 assemble(a, c)
-            else:
-                got(big.at[a, rows(oi, c)], grecv.at[a, oi, c])
             src = big.at[a, rows(oi, c)]
             if j == 0:
                 for kid, way in KIDS[i]:
                     to = OI[kid, 0]
-                    rc(src, big.at[a, rows(to, c)], gsend.at[a], grecv.at[a, to, c],
+                    rc(src, big.at[a, rows(to, c)], gsend.at[a], grecv.at[sem_of(GATHER_SEM, a, to, c)],
                        xz_dev(c, 0, way)).start()
             if oi:
                 along_second(a, oi, c)
@@ -209,14 +214,14 @@
         full[half_rows(k, mine), :] = s
         out[k] = s.astype(BF)
         for w, way in ((0, 1), (1, -1)):
-            rc(out.at[k, pl.ds(w * 64, 64)], relay.at[k, w], e1s.at[a], e1r.at[a, k, w],
+            rc(out.at[k, pl.ds(w * 64, 64)], relay.at[k, w], e1s.at[a], e1r.at[a, k],
                y_dev(way + 4)).start()
 
     def relay_on(a, k):
         _, _, _, relay, recv = part[a]
+        got(relay.at[k], e1r.at[a, k])
         for w, way in ((0, 1), (1, -1)):
-            got(relay.at[k, w], e1r.at[a, k, w])
-            rc(relay.at[k, w], recv.at[k, pl.ds(w * 64, 64)], e2s.at[a], e2r.at[a, k, w],
+            rc(relay.at[k, w], recv.at[k, pl.ds(w * 64, 64)], e2s.at[a], e2r.at[a, k],
                y_dev(way + 4)).start()
 
     def total(a, k, cols):
@@ -224,9 +229,7 @@
         return full[half_rows(k, mine), cols] + recv[k, :, cols].astype(F32)
 
     def arrived(a, k):
-        recv = part[a][4]
-        for w in range(2):
-            got(recv.at[k, pl.ds(w * 64, 64)], e2r.at[a, k, w])
+        got(part[a][4].at[k], e2r.at[a, k])
 
     def forward_act(k):
         arrived(0, k)
@@ -282,13 +285,12 @@
         if j == 0:
             kids += [OI[kid, 0] for kid, _ in KIDS[i]]
         if oi:
-            along = j or i
-            parent, way = next((p, w) for p in KIDS for q, w in KIDS[p] if q == along)
-            above, axis = ((i, parent), 1) if j else ((parent, 0), 0)
+            way = next(w for p in KIDS for q, w in KIDS[p] if q == (j or i))
+            axis = 1 if j else 0
 
         def send(c):
             rc(par.at[a, rows(oi, c)], rin.at[a, rows(oi, c)], rsend.at[a],
-               rrecv.at[a, oi, c], xz_dev(c, axis, -way)).start()
+               rrecv.at[sem_of(REDUCE_SEM, a, oi, c)], xz_dev(c, axis, -way)).start()
 
         if which:
             leaf = LEAVES.index((i, j)) if (i, j) in LEAVES else None
@@ -296,25 +298,30 @@
             @pl.loop(0, 2)
             def _(n):
                 rc(par.at[a, rows(oi, its(n))], pex.at[a, leaf, n], qsend.at[a],
-                   qrecv.at[a, leaf, n], pair).start()
+                   qrecv.at[a, leaf], pair).start()
             return
         if which == "x":
+            got(pex.at[a, leaf], qrecv.at[a, leaf])
+
             @pl.loop(0, 2)
             def _(n):
                 c = ours(n)
-                got(pex.at[a, leaf, n], qrecv.at[a, leaf, n])
                 par[a, rows(oi, c), :] = (
                     par[a, rows(oi, c), :].astype(F32) + pex[a, leaf, n].astype(F32)
                 ).astype(BF)
                 send(c)
             return
         if which == "k":
+            got(rin.at[a, pl.ds(oi * 64, 32)], rrecv.at[REDUCE_SEM[a, oi][0]])
+
             @pl.loop(0, 2)
             def _(n):
                 c = ours(n)
-                got(rin.at[a, rows(oi, c)], rrecv.at[a, oi, c])
-                keep[a, rows(KEPT.index(above), c), :] += rin[a, rows(oi, c), :].astype(F32)
+                keep[a, rows(KEPT.index(above(oi)), c), :] += rin[a, rows(oi, c), :].astype(F32)
             return
+
+        for kid in kids:
+            got_blocks(REDUCE_SEM, rrecv, rin, a, kid, which)
 
         @pl.loop(*COLOURS[which])
         def _(n):
@@ -322,32 +329,41 @@
             if (i, j) in KEPT:
                 acc = keep[a, rows(KEPT.index((i, j)), c), :]
                 for kid in kids:
-                    got(rin.at[a, rows(kid, c)], rrecv.at[a, kid, c])
                     acc += rin[a, rows(kid, c), :].astype(F32)
                 if oi:
                     par[a, rows(oi, c), :] = acc.astype(BF)
                 else:
                     for h in range(2):
                         g = c * 2 + h
-                        yse[a, g] = acc[h * 8 : h * 8 + 8]
-
-                        @pl.when(g != f)
+                        piece = acc[h * 8 : h * 8 + 8]
+                        far = c == (y + 2) % 4
+
+                        @pl.when(far)
                         def _():
-                            rc(yse.at[a, g], yor.at[a, f], fsend.at[a], frecv.at[a, f],
+                            far_out[a, h] = piece.astype(BF)
+                            rc(far_out.at[a, h], far_in.at[a, co], fsend.at[a, 1], frecv.at[a, 1],
+                               ring_dev(g)).start()
+
+                        @pl.when(jnp.logical_not(far))
+                        def _():
+                            yse[a, g] = piece
+
+                        @pl.when(jnp.logical_not(far | (g == f)))
+                        def _():
+                            rc(yse.at[a, g], yor.at[a, f], fsend.at[a, 0], frecv.at[a, 0],
                                ring_dev(g)).start()
             if oi:
                 send(c)
 
     def finish(a):
         yor[a, f] = yse[a, f]
-
-        @pl.loop(1, 8)
-        def _(k):
-            g = (f + k) % 8
-            got(yor.at[a, g], frecv.at[a, g])
+        got(yor.at[a, pl.ds(0, 5)], frecv.at[a, 0])
+        got(far_in.at[a], frecv.at[a, 1])
+        for h in range(2):
+            yor[a, ((y + 2) % 4) * 2 + h] = far_in[a, h].astype(F32)
 
     def down_piece(n):
-        cols = pl.ds(n * 256, 256)
+        cols = pl.ds(n * 1024, 1024 - 256 * n)
         sdg[:, cols] = lax.dot_general(
             hid[...], big[1, :, cols], (((0,), (0,)), ((), ())), preferred_element_type=F32
         )
@@ -379,14 +395,12 @@
         "FI": finish,
     }
     for word in PROGRAM:
-        name = word.rstrip("abcdkxy").rstrip("0123456789")
-        number = word[len(name):].rstrip("abcdkxy")
-        which = word[len(name) + len(number):]
+        name, number, which = split_word(word)
         with jax.named_scope(word):
             if name in ("T", "C", "RM", "RI"):
-                steps[name](int(number), which)
+                steps[name](number, which)
             else:
-                steps[name](int(number))
+                steps[name](number)
 
     for a in range(2):
         sent(yin.at[a, pl.ds(0, 7)], ysend.at[a])
@@ -398,23 +412,59 @@
         shared = len(REDUCE_SHARED[a])
         sent(pex.at[a, pl.ds(0, shared)], qsend.at[a])
         sent(par.at[a, pl.ds(0, 15 * 64 - 32 * shared)], rsend.at[a])
-        sent(yse.at[a, pl.ds(0, 7)], fsend.at[a])
+        sent(yse.at[a, pl.ds(0, 5)], fsend.at[a, 0])
+        sent(far_out.at[a], fsend.at[a, 1])
 
 
 PROGRAM = (
-    "T0a", "T0c", "T4a", "T0d", "T1a", "T2a", "T3a", "T1b", "T3b", "T2b", "GU0", "T5",
-    "T6", "S0", "T4b", "T7", "GU1", "T10", "S1", "T9", "T8", "T11", "GU2", "T14",
-    "C0", "R0", "T12", "S2", "T13", "R1", "T15", "GU3", "H0", "C3", "S3", "C1",
-    "C2", "R2", "H1", "B0", "R3", "M0", "RM4", "SB0", "C5", "C7", "C4", "C6",
-    "B1", "H2", "H3", "C9", "SB1", "RB0", "C10", "M1", "RM10y", "C11", "RM15", "RM13y",
-    "RM12", "C14", "RM9", "C13", "RM14", "RB1", "C12", "C8", "DB0", "B2", "C15", "B3",
-    "SB2", "RM11", "SB3", "RM6", "DB1", "RM13x", "RB2", "RM8", "WD0", "RB3", "RM5", "RM10x",
-    "I0", "DB2", "RM2", "DB3", "RM13k", "RM7", "RI4y", "RM1", "I1", "RI15", "RI13y", "WD4",
-    "RI9y", "RI12", "RM10k", "RM3", "RI14", "RI10y", "WG3", "WD5", "RI11", "RI6", "WD2", "RI13x",
-    "RI8", "RM0", "RI4x", "RI9x", "WG5", "RI5b", "WD1", "RI10x", "WG4", "RI13k", "RI7", "WD3",
-    "RI4k", "RI5a", "WD6", "RI9k", "RI2b", "RI2a", "RI1b", "RI10k", "RI3b", "WG2", "RI1a", "RI0d",
-    "WG1", "RI0c", "FM0", "RI3a", "WG0", "RI0a", "WG6", "FI1",
+    "T0a", "C0a", "T1a", "T0c", "T0d", "C0b", "T1b", "T3a", "T4b", "T3b", "T4a", "T2b",
+    "T2a", "GU0", "S0", "T5", "T6", "T7", "GU1", "T8", "T10", "T9", "R0", "S1",
+    "T11", "GU2", "C1", "T14", "T13", "C3", "T12", "C2", "S2", "T15", "GU3", "R1",
+    "S3", "C5", "H0", "R2", "C6", "C4", "B0", "H1", "C7", "R3", "M0", "C11",
+    "C8", "C9", "C10", "B1", "RM4", "H2", "B2", "C13", "C12", "SB1", "C14", "H3",
+    "SB2", "C15", "B3", "SB0", "M1", "RM15", "SB3", "RM12", "RM9", "RB1", "RM14", "WD1",
+    "RB2", "RB3", "RB0", "RM11", "RM6", "RM8", "RM10y", "DB2", "DB3", "RM13y", "RM2", "RM5",
+    "I1", "RI15", "RI8", "RI13y", "RM10x", "DB1", "RI10y", "RI12", "DB0", "RM13x", "RM1", "RI11",
+    "I0", "WG4", "RI14", "WG1", "RI13x", "RM13k", "RM7", "RI10x", "RI6", "WG6", "WD0", "RI5",
+    "RI13k", "RI7", "RM10k", "WG0", "RM3", "WG5", "RI10k", "RI9", "WG3", "RI4", "WG2", "RI3a",
+    "RI3b", "RI1b", "RM0", "RI2b", "RI0d", "RI2a", "RI1a", "RI0c", "RI0a", "FM0", "FI1",
 )
+
+
+COLOURS = {"": (0, 4), "a": (0, 1), "b": (1, 4), "c": (1, 3), "d": (3, 4)}
+
+
+def split_word(word):
+    name = word.rstrip("abcdkxy").rstrip("0123456789")
+    number = word[len(name):].rstrip("abcdkxy")
+    return name, int(number), word[len(name) + len(number):]
+
+
+def parts_of(name, oi):
+    which = {w for a, n, w in map(split_word, PROGRAM) if a == name and n == oi}
+    return 3 if "d" in which else 2 if "a" in which else 1
+
+
+def above(oi):
+    i, j = IJ[oi]
+    up = next(p for p in KIDS for q, _ in KIDS[p] if q == (j or i))
+    return (i, up) if j else (up, 0)
+
+
+def tables():
+    gather, reduce, at = {}, {}, [0, 0]
+    for a in range(2):
+        for oi in range(1, 16):
+            n = parts_of("TC"[a], oi)
+            gather[a, oi] = at[0], n
+            at[0] += n
+            n = 1 if IJ[oi] in REDUCE_SHARED[a] else parts_of(("RM", "RI")[a], OI[above(oi)])
+            reduce[a, oi] = at[1], n
+            at[1] += n
+    return gather, reduce, at
+
+
+GATHER_SEM, REDUCE_SEM, SEMS = tables()
 
 
 def write_out(sgu, sdg, yor, mixed, igrad, gg, ug, dg, rows, sem):
@@ -475,16 +525,18 @@
             pltpu.VMEM((2, T, DB), BF),
             pltpu.VMEM((2, 4, 2, 16, DB), BF),
             pltpu.VMEM((2, 8, 8, DB), F32),
-            dma((2,)), dma((2, 8)),
-            dma((2,)), dma((2, 16, 4)),
+            pltpu.VMEM((2, 2, 8, DB), BF),
+            pltpu.VMEM((2, 2, 8, DB), BF),
+            dma((2,)), dma((2, 3)),
+            dma((2,)), dma((SEMS[0],)),
             dma((5,)),
             dma((2,)), dma((2, 4)),
-            dma((2,)), dma((2, 4, 2)),
-            dma((2,)), dma((2, 4, 2)),
             dma((2,)), dma((2, 4)),
-            dma((2,)), dma((2, 16, 4)),
-            dma((2,)), dma((2, 8)),
-            dma((2,)), dma((2, 4, 2)),
+            dma((2,)), dma((2, 4)),
+            dma((2,)), dma((2, 4)),
+            dma((2,)), dma((SEMS[1],)),
+            dma((2, 2)), dma((2, 2)),
+            dma((2,)), dma((2, 4)),
         ],
         compiler_params=pltpu.CompilerParams(
             collective_id=0, has_side_effects=True, vmem_limit_bytes=53 * 1024 * 1024

time: 100 us -> 98.4 us (0.984)
  Pallas kernels: 98.3 us -> 96.2 us
    pallas_call x1, Pallas kernels: 94.9 us -> 92.8 us  [body(): pl.pallas_call(kernel, name='ffn', out_shape=(pltpu.VMEM((DB, 2 * H), F32...]
where the time goes in v3:
time: 98.4 us; the launch traced here: 97 us
  Pallas kernels  96.2 us (98%)
    pallas_call x1, Pallas kernels, body(): pl.pallas_call(kernel, name='ffn', out_shape=(pltpu.VMEM((DB, 2 * H), F32...  92.8 us
    pallas_call x1, Pallas kernels, body(): pl.pallas_call(write_out, name='write_out', out_shape=(jax.ShapeDtypeStru...  3.4 us

profile of v3, /device:TPU:0, one launch (start us, length us, event | category | flops | bytes accessed | tf_op | source)
XLA Modules:
  0.0 97.0 jit_solution(7441524447214754876)
XLA Ops:
  0.6 92.8 %ffn.1 = (f32[1792,768]{1,0:T(8,128)S(1)}, f32[384,1792]{1,0:T(8,128)S(1)}, f32[2,8,8,1792]{3,2,1,0:T(8,128)S(1)}) custom-call(bf16[8,7168]{1,0:T(8,128)(2,1)} %tok_in.1, bf16[8,7168]{1,0:T(8,128)(2,1)} %cot_in.1, bf16[7168,384]{1,0:T(8,128)(2,1)} %wg.1, bf16[7168,384]{1,0:T(8,128)(2,1)} %wu.1, bf16[384,7168]{1,0:T(8,128)(2,1)} %wd.1), custom_call_target="tpu_custom_call" | custom-call | tf_op jit(solution)/shard_map/ffn/pallas_call | solution.py:492
  93.4 3.4 %write_out.1 = (bf16[8,7168]{1,0:T(8,128)(2,1)}, bf16[8,7168]{1,0:T(8,128)(2,1)}, f32[1792,384]{1,0:T(8,128)}, f32[1792,384]{1,0:T(8,128)}, f32[384,1792]{1,0:T(8,128)}) custom-call(f32[1792,768]{1,0:T(8,128)S(1)} %get-tuple-element.8.sgu, f32[384,1792]{1,0:T(8,128)S(1)} %get-tuple-element.9.sdg, f32[2,8,8,1792]{3,2,1,0:T(8,128)S(1)} %get-tuple-element.10.yor), custom_call_target="tpu_custom_call" | custom-call | tf_op jit(solution)/shard_map/write_out/pallas_call | solution.py:545

commit v4 on v3

--- a/solution.py
+++ b/solution.py
@@ -374,7 +374,20 @@
             big[0, :, r], dgu[...], (((0,), (0,)), ((), ())), preferred_element_type=F32
         )
 
+    def all_sent(a):
+        sent(yin.at[a, pl.ds(0, 7)], ysend.at[a])
+        sent(big.at[a, pl.ds(0, 15 * 64)], gsend.at[a])
+        sent(part[a][1], d1s.at[a])
+        sent(part[a][3], e1s.at[a])
+        sent(part[a][3], e2s.at[a])
+        sent((hid, dgu)[a].at[pl.ds(0, T // 2)], d2s.at[a])
+        if a == 0:
+            shared = len(REDUCE_SHARED[a])
+            sent(pex.at[a, pl.ds(0, shared)], qsend.at[a])
+            sent(par.at[a, pl.ds(0, 15 * 64 - 32 * shared)], rsend.at[a])
+
     steps = {
+        "Z": all_sent,
         "T": functools.partial(gather_step, 0),
         "C": functools.partial(gather_step, 1),
         "GU": functools.partial(product, 0),
@@ -403,15 +416,10 @@
                 steps[name](number)
 
     for a in range(2):
-        sent(yin.at[a, pl.ds(0, 7)], ysend.at[a])
-        sent(big.at[a, pl.ds(0, 15 * 64)], gsend.at[a])
-        sent(part[a][1], d1s.at[a])
-        sent(part[a][3], e1s.at[a])
-        sent(part[a][3], e2s.at[a])
-        sent((hid, dgu)[a].at[pl.ds(0, T // 2)], d2s.at[a])
         shared = len(REDUCE_SHARED[a])
-        sent(pex.at[a, pl.ds(0, shared)], qsend.at[a])
-        sent(par.at[a, pl.ds(0, 15 * 64 - 32 * shared)], rsend.at[a])
+        if a:
+            sent(pex.at[a, pl.ds(0, shared)], qsend.at[a])
+            sent(par.at[a, pl.ds(0, 15 * 64 - 32 * shared)], rsend.at[a])
         sent(yse.at[a, pl.ds(0, 5)], fsend.at[a, 0])
         sent(far_out.at[a], fsend.at[a, 1])
 
@@ -427,7 +435,7 @@
     "I1", "RI15", "RI8", "RI13y", "RM10x", "DB1", "RI10y", "RI12", "DB0", "RM13x", "RM1", "RI11",
     "I0", "WG4", "RI14", "WG1", "RI13x", "RM13k", "RM7", "RI10x", "RI6", "WG6", "WD0", "RI5",
     "RI13k", "RI7", "RM10k", "WG0", "RM3", "WG5", "RI10k", "RI9", "WG3", "RI4", "WG2", "RI3a",
-    "RI3b", "RI1b", "RM0", "RI2b", "RI0d", "RI2a", "RI1a", "RI0c", "RI0a", "FM0", "FI1",
+    "RI3b", "RI1b", "RM0", "RI2b", "Z0", "Z1", "RI0d", "RI2a", "RI1a", "RI0c", "RI0a", "FM0", "FI1",
 )
 
 

time: 98.4 us -> 98.4 us (level)
  no operation moved by 1% of the time
where the time goes in v4:
time: 98.4 us; the launch traced here: 96.9 us
  Pallas kernels  96.1 us (98%)
    pallas_call x1, Pallas kernels, body(): pl.pallas_call(kernel, name='ffn', out_shape=(pltpu.VMEM((DB, 2 * H), F32...  92.7 us
    pallas_call x1, Pallas kernels, body(): pl.pallas_call(write_out, name='write_out', out_shape=(jax.ShapeDtypeStru...  3.4 us

profile of v4, /device:TPU:0, one launch (start us, length us, event | category | flops | bytes accessed | tf_op | source)
XLA Modules:
  0.0 96.9 jit_solution(16177855558360105951)
XLA Ops:
  0.6 92.7 %ffn.1 = (f32[1792,768]{1,0:T(8,128)S(1)}, f32[384,1792]{1,0:T(8,128)S(1)}, f32[2,8,8,1792]{3,2,1,0:T(8,128)S(1)}) custom-call(bf16[8,7168]{1,0:T(8,128)(2,1)} %tok_in.1, bf16[8,7168]{1,0:T(8,128)(2,1)} %cot_in.1, bf16[7168,384]{1,0:T(8,128)(2,1)} %wg.1, bf16[7168,384]{1,0:T(8,128)(2,1)} %wu.1, bf16[384,7168]{1,0:T(8,128)(2,1)} %wd.1), custom_call_target="tpu_custom_call" | custom-call | tf_op jit(solution)/shard_map/ffn/pallas_call | solution.py:500
  93.4 3.4 %write_out.1 = (bf16[8,7168]{1,0:T(8,128)(2,1)}, bf16[8,7168]{1,0:T(8,128)(2,1)}, f32[1792,384]{1,0:T(8,128)}, f32[1792,384]{1,0:T(8,128)}, f32[384,1792]{1,0:T(8,128)}) custom-call(f32[1792,768]{1,0:T(8,128)S(1)} %get-tuple-element.8.sgu, f32[384,1792]{1,0:T(8,128)S(1)} %get-tuple-element.9.sdg, f32[2,8,8,1792]{3,2,1,0:T(8,128)S(1)} %get-tuple-element.10.yor), custom_call_target="tpu_custom_call" | custom-call | tf_op jit(solution)/shard_map/write_out/pallas_call | solution.py:553
